TPU v7x, 32 devices: a whole 2x2x4 slice. The times are simulated.
32 devices in a mesh: cls: 4 (over y, x), org: 8 (over z, core).
Axes of the slice: x: 2, y: 2, z: 4, core: 2. Of those that a mesh axis runs over, the one named last changes fastest.
Arguments:
- flows_start: float32 [8, 49152], P('cls', 'org'), may hold values from 150 to 300
- interaction: float32 [8, 8, 49152], P('cls', None, 'org'), may hold values from 0.2 to 2
- free_time: float32 [8, 49152], P('cls', 'org'), may hold values from 0.01 to 0.1
- capacity: float32 [49152], P('org'), may hold values from 300 to 900
- demand: int32 [8, 8, 60], P('cls', 'org'), may hold values from 0 to 15
- incidence: int32 [2, 8, 8, 2, 49152], P(None, 'cls', 'org'), may hold values from 0 to 1073741823, as said below
- step_size: float32 [2], replicated, may hold values from 0.3 to 0.6
Outputs:
- flows: float32 [8, 49152], P('cls', 'org')
- costs: float32 [8, 49152], P('cls', 'org')
- skims: float32 [2, 8, 8, 60], P(None, 'cls', 'org')
- gaps: float32 [2], replicated
Inputs may be any that keep to these rules, and one draw needn't show every extreme that they name: Bit b of incidence[k, c, o, w, l] tells whether link l lies on class c's path from anchor o to destination w * 30 + b in iteration k; each path is the union of 4 runs of 64 consecutive links (counted cyclically over the links) at drawn starts, the first of which is shared by all 30 destinations of one word.
All inputs are finite; a program needn't handle non-finite values.
Results may differ from a plain program's by a relative error of at most 0.0013.
Values sent between devices are 32-bit elements; how exact they have to be, the bound alone decides.
A program may use at most 256 MiB of HBM per device.

v0:
```python
import jax
import jax.numpy as jnp
from jax import lax
from jax.sharding import PartitionSpec as P

BITS = 30
ITERS = 2
HIGH = lax.Precision.HIGHEST


def unpack_half(packed):
    shifts = jnp.arange(BITS, dtype=jnp.int32)
    bit_table = jnp.bitwise_and(jnp.right_shift(packed[..., :, None, :], shifts[:, None]), 1)
    new_shape = packed.shape[:-2] + (packed.shape[-2] * BITS, packed.shape[-1])
    return bit_table.reshape(new_shape).astype(jnp.bfloat16)


def link_cost(flows_all, inter, free, cap):
    load_sum = jnp.einsum("cel,el->cl", inter, flows_all, precision=HIGH)
    load_ratio = load_sum / cap
    square = load_ratio * load_ratio
    return free * (1.0 + 0.15 * square * square)


def split_three(values):
    upper = values.astype(jnp.bfloat16)
    remain = values - upper.astype(jnp.float32)
    middle = remain.astype(jnp.bfloat16)
    lowest = (remain - middle.astype(jnp.float32)).astype(jnp.bfloat16)
    return jnp.stack([upper, middle, lowest], axis=1)


def skim_block(bit_table, cost_block):
    parts = split_three(cost_block)
    terms = jnp.einsum("codl,cpl->cpod", bit_table, parts, preferred_element_type=jnp.float32)
    return jnp.sum(terms, axis=1)


def anchor_loads_local(packed_all, trips_half, link_shard, block_count):

    def one_block(block_index):
        word_block = lax.dynamic_slice_in_dim(packed_all, block_index * link_shard, link_shard, 3)
        bit_table = unpack_half(word_block)
        return jnp.einsum("cod,codl->cl", trips_half, bit_table, preferred_element_type=jnp.float32)

    blocks = lax.map(one_block, jnp.arange(block_count, dtype=jnp.int32))
    return jnp.moveaxis(blocks, 0, 1).reshape(blocks.shape[1], block_count * link_shard)


def make_fold(packed_all, link_shard):

    def fold_links(skim_carry, portion, first):
        turn_count = portion.shape[1] // link_shard

        def advance(skim_sum, block_index):
            offset = block_index * link_shard
            word_block = lax.dynamic_slice_in_dim(packed_all, offset, link_shard, 3)
            bit_table = unpack_half(word_block)
            cost_block = lax.dynamic_slice_in_dim(portion, offset, link_shard, 1)
            return (skim_sum + skim_block(bit_table, cost_block), None)

        result, unused = lax.scan(advance, skim_carry, jnp.arange(turn_count, dtype=jnp.int32))
        return result

    return fold_links


def both_totals(cost_part, path_part):
    return lax.psum((cost_part, path_part), ("cls", "org"))


def shards(flows_start, interaction, free_time, capacity, demand, incidence, step_size):
    org_count = lax.axis_size("org")
    link_shard = flows_start.shape[1]
    dest_count = demand.shape[2]
    class_local = demand.shape[0]
    demand_real = demand.astype(jnp.float32)
    trips_half = demand.astype(jnp.bfloat16)
    own_start = lax.axis_index("org") * link_shard
    skim_init = jnp.zeros((class_local, demand.shape[1], dest_count), jnp.float32)
    skim_list = []
    gap_list = []
    inter_full, free_full, cap_full, flow_now = (
        lax.all_gather(interaction, "org", axis=2, tiled=True),
        lax.all_gather(free_time, "org", axis=1, tiled=True),
        lax.all_gather(capacity, "org", axis=0, tiled=True),
        lax.all_gather(flows_start, "org", axis=1, tiled=True),
    )

    def full_cost(flow_value):
        flows_all = lax.all_gather(flow_value, "cls", axis=0, tiled=True)
        return link_cost(flows_all, inter_full, free_full, cap_full)

    for iteration in range(ITERS):
        cost_now = full_cost(flow_now)
        fold_links = make_fold(incidence[iteration], link_shard)
        skim_now = fold_links(skim_init, cost_now, jnp.int32(0))
        partial_value = anchor_loads_local(incidence[iteration], trips_half, link_shard, org_count)
        aon = lax.psum(partial_value, "org")
        product = lax.dynamic_slice_in_dim(cost_now * flow_now, own_start, link_shard, 1)
        cost_total, path_total = both_totals(jnp.sum(product), jnp.sum(demand_real * skim_now))
        gap_list.append((cost_total - path_total) / cost_total)
        skim_list.append(skim_now)
        flow_now = flow_now + step_size[iteration] * (aon - flow_now)
    cost_final = full_cost(flow_now)
    flow_out = lax.dynamic_slice_in_dim(flow_now, own_start, link_shard, 1)
    cost_out = lax.dynamic_slice_in_dim(cost_final, own_start, link_shard, 1)
    return (flow_out, cost_out, jnp.stack(skim_list), jnp.stack(gap_list))


def solution(mesh):
    placed = (
        P("cls", "org"),
        P("cls", None, "org"),
        P("cls", "org"),
        P("org"),
        P("cls", "org", None),
        P(None, "cls", "org", None, None),
        P(),
    )
    return jax.shard_map(
        shards,
        mesh=mesh,
        in_specs=placed,
        out_specs=(P("cls", "org"), P("cls", "org"), P(None, "cls", "org", None), P()),
        check_vma=False,
    )
```

profile of v0, /device:TPU:0, one launch (start us, length us, event | category | flops | bytes accessed | tf_op | source)
XLA Modules:
  0.0 387.4 jit_solution(10713880894416797273)
XLA Ops:
  10.9 32.3 %while.43 = (s32[]{:T(128)}, f32[8,2,6144]{2,1,0:T(2,128)S(1)}, s32[8]{0:T(128)S(1)}, s32[2,1,2,49152]{3,0,2,1:T(2,128)S(1)}, bf16[2,1,60]{2,0,1:T(2,128)(2,1)S(...) while((s32[]{:T(128)}, f32[8,2,6144]{2,1,0:T(2,128)S(1)}, s32[8]{0:T(128)S(1)}, ...), condition=%wide.region_4.5_spmd, body=%wide.region_3.4_spmd.sunk | while | flops 3686406 | bytes 3392847 | solution.py:46
  12.3 1.7 fusion.83
  16.3 1.7 fusion.83
  20.3 1.7 fusion.83
  24.4 1.7 fusion.83
  28.4 1.7 fusion.83
  32.5 1.7 fusion.83
  36.5 1.7 fusion.83
  40.5 1.7 fusion.83
  44.3 32.3 %while.42 = (s32[]{:T(128)}, f32[8,2,6144]{2,1,0:T(2,128)S(1)}, s32[8]{0:T(128)S(1)}, s32[2,1,2,49152]{3,0,2,1:T(2,128)S(1)}, bf16[2,1,60]{2,0,1:T(2,128)(2,1)S(...) while((s32[]{:T(128)}, f32[8,2,6144]{2,1,0:T(2,128)S(1)}, s32[8]{0:T(128)S(1)}, ...), condition=%wide.region_1.0_spmd, body=%wide.region_0.1_spmd.sunk | while | flops 3686406 | bytes 3392847 | solution.py:46
  45.7 1.7 fusion.79
  49.7 1.7 fusion.79
  53.8 1.7 fusion.79
  57.8 1.7 fusion.79
  61.8 1.7 fusion.79
  65.9 1.7 fusion.79
  69.9 1.7 fusion.79
  74.0 1.7 fusion.79
  77.5 17.5 %all_gather.21 = f32[2,49152]{1,0:T(2,128)} all-gather(f32[2,6144]{1,0:T(2,128)S(1)} %copy-done.7), channel_id=1, replica_groups=mesh['cls'=4,'org'=8] {'org'}, dimensions={1}, use_global_device_ids=true | all-gather | bytes 442368 | tf_op jit(solution)/shard_map/all_gather | solution.py:87
  95.7 42.7 %all-reduce.4.cloned.1.call-done = (f32[2,49152]{1,0:T(2,128)}, f32[2,49152]{1,0:T(2,128)}) async-done(((f32[2,49152]{1,0:T(2,128)}, f32[2,49152]{1,0:T(2,128)}), (f32[2,49152]{1,0:T(2,128)}, f32[2,49152]{1,0:T(2,128)})) %all-reduce.4.cloned.1.call-update) | async-done | bytes 786448 | tf_op jit(solution)/shard_map/psum | solution.py:99
  138.4 3.8 multiply_add_fusion
  143.5 15.2 %all_gather.25 = f32[49152]{0:T(1024)} all-gather(f32[6144]{0:T(1024)S(1)} %copy-done.9), channel_id=1, replica_groups=mesh['cls'=4,'org'=8] {'org'}, dimensions={0}, use_global_device_ids=true | all-gather | bytes 221184 | tf_op jit(solution)/shard_map/all_gather | solution.py:86
  158.7 14.7 %all_gather.22 = f32[2,49152]{1,0:T(2,128)S(1)} all-gather(f32[2,6144]{1,0:T(2,128)S(1)} %copy-done.8), channel_id=1, replica_groups=mesh['cls'=4,'org'=8] {'org'}, dimensions={1}, use_global_device_ids=true | all-gather | bytes 442368 | tf_op jit(solution)/shard_map/all_gather | solution.py:85
  174.8 2.5 reshape.94
  177.3 2.5 reshape.92
  179.8 24.8 %all-gather.14.cloned.1.call-done = f32[4,2,49152]{2,1,0:T(2,128)} async-done(((f32[1,2,49152]{2,1,0:T(2,128)}), f32[4,2,49152]{2,1,0:T(2,128)}) %all-gather.14.cloned.1.call-update) | async-done | bytes 1572880 | tf_op jit(solution)/shard_map/all_gather | solution.py:91
  204.6 3.6 reshape.96
  208.2 36.0 %all-gather.8.cloned.1.call-done = f32[2,8,49152]{2,1,0:T(8,128)} async-done(((f32[2,8,6144]{2,1,0:T(8,128)}), f32[2,8,49152]{2,1,0:T(8,128)}) %all-gather.8.cloned.1.call-update) | async-done | bytes 3145744 | tf_op jit(solution)/shard_map/all_gather | solution.py:84
  244.2 6.9 %multiply_reduce_fusion.1 = (f32[49152,2]{0,1:T(2,128)S(1)}, f32[49152,2]{0,1:T(2,128)S(1)}, f32[49152,2]{0,1:T(2,128)}) fusion(f32[2,8,49152]{2,1,0:T(8,128)} %all-gather.8.cloned.1.call-done, f32[49152,8]{0,1:T(8,128)S(1)} %bitcast.155, f32[49152,8]{0,1:T(8,128)} %bitcast.157, f32[49152,8]{0,1:T(8,128)S(1)} %bitcast.156), kind=kLoop, calls=%fused_computation.59 | loop fusion | flops 4423680 | bytes 9043968 | tf_op jit(solution)/shard_map/cel,el->cl/dot_general | solution.py:19
  253.4 39.4 %while.44 = (s32[]{:T(128)}, f32[2,1,60]{2,0,1:T(2,128)S(1)}, s32[8]{0:T(128)S(1)}, f32[2,49152]{1,0:T(2,128)S(1)}, s32[2,1,2,49152]{3,0,2,1:T(2,128)}, /*index=5*/s32[]{:T(128)}, s32[1]{0:T(128)}, s32[]{:T(128)}, s32[]{:T(128)}) while((s32[]{:T(128)}, f32[2,1,60]{2,0,1:T(2,128)S(1)}, s32[8]{0:T(128)S(1)}, ...), condition=%wide.region_8.9_spmd.clone, body=%wide.region_6.8_spmd.clone.sunk | while | flops 6943207 | bytes 3615725 | solution.py:62
  255.9 1.7 fusion.87
  260.8 1.7 fusion.87
  265.7 1.7 fusion.87
  270.6 1.7 fusion.87
  275.5 1.7 fusion.87
  280.5 1.7 fusion.87
  285.4 1.7 fusion.87
  290.3 1.7 fusion.87
  294.2 39.4 %while.45 = (s32[]{:T(128)}, f32[2,1,60]{2,0,1:T(2,128)S(1)}, s32[8]{0:T(128)S(1)}, f32[2,49152]{1,0:T(2,128)S(1)}, s32[2,1,2,49152]{3,0,2,1:T(2,128)}, /*index=5*/s32[]{:T(128)}, s32[1]{0:T(128)}, s32[]{:T(128)}, s32[]{:T(128)}) while((s32[]{:T(128)}, f32[2,1,60]{2,0,1:T(2,128)S(1)}, s32[8]{0:T(128)S(1)}, ...), condition=%wide.region_11.12_spmd.clone, body=%wide.region_9.11_spmd.clone.sunk | while | flops 6943207 | bytes 3615725 | solution.py:62
  296.7 1.7 fusion.93
  301.6 1.7 fusion.93
  306.5 1.7 fusion.93
  311.5 1.7 fusion.93
  316.4 1.7 fusion.93
  321.3 1.7 fusion.93
  326.2 1.7 fusion.93
  331.1 1.7 fusion.93
  334.2 39.7 %all-reduce = (f32[]{:T(128)}, f32[]{:T(128)}, f32[]{:T(128)}, f32[]{:T(128)}) all-reduce(f32[]{:T(128)} %fusion.53, f32[]{:T(128)} %get-tuple-element.186, f32[]{:T(128)} %fusion.54, f32[]{:T(128)} %get-tuple-element.185), channel_id=1, replica_groups=mesh['cls'=4,'org'=8] {'cls','org'}, use_global_device_ids=true, to_apply=%region_17.18 | all-reduce | flops 4 | bytes 32 | tf_op jit(solution)/shard_map/psum | solution.py:69
  (329 shorter events, 79.8 us)
Async XLA Ops:
  8.0 130.4 %all-reduce.4.cloned.1.call-start = ((), (), s32[]{:S(2)}) async-start(), calls=%async_computation.4 | async-start | bytes 1572864 | tf_op jit(solution)/shard_map/psum | solution.py:99
  8.0 1.5 copy-start.11
  43.2 1.0 copy-start
  43.2 1.1 copy-start.6
  43.3 34.1 %copy-start.7 = (f32[2,6144]{1,0:T(2,128)S(1)}, f32[2,6144]{1,0:T(2,128)}, u32[]{:S(2)}) copy-start(f32[2,6144]{1,0:T(2,128)} %param.15) | copy-start | bytes 147460
  76.6 0.8 copy-start.5
  76.6 65.5 %copy-start.1 = (s32[2,1,2,49152]{3,0,2,1:T(2,128)}, s32[2,1,2,49152]{3,0,2,1:T(2,128)S(1)}, u32[]{:S(2)}) copy-start(s32[2,1,2,49152]{3,0,2,1:T(2,128)S(1)} %get-tuple-element.496) | copy-start | bytes 2359300
  76.6 18.4 %copy-start.10 = (f32[2]{0:T(128)S(1)}, f32[2]{0:T(128)}, u32[]{:S(2)}) copy-start(f32[2]{0:T(128)} %param.21) | copy-start | bytes 28
  77.4 97.4 %all-gather.12.cloned.1.call-start = ((), (), s32[]{:S(2)}) async-start(), calls=%async_computation.2 | async-start | bytes 1966080 | tf_op jit(solution)/shard_map/all_gather | solution.py:91
  95.0 82.3 %all-gather.10.cloned.1.call-start = ((), (), s32[]{:S(2)}) async-start(), calls=%async_computation.1 | async-start | bytes 1966080 | tf_op jit(solution)/shard_map/all_gather | solution.py:91
  138.4 5.1 %copy-start.9 = (f32[6144]{0:T(1024)S(1)}, f32[6144]{0:T(1024)}, u32[]{:S(2)}) copy-start(f32[6144]{0:T(1024)} %param.18) | copy-start | bytes 73732
  138.4 20.3 %copy-start.8 = (f32[2,6144]{1,0:T(2,128)S(1)}, f32[2,6144]{1,0:T(2,128)}, u32[]{:S(2)}) copy-start(f32[2,6144]{1,0:T(2,128)} %param.17) | copy-start | bytes 147460
  142.2 62.4 %all-gather.14.cloned.1.call-start = ((), (), s32[]{:S(2)}) async-start(), calls=%async_computation.3 | async-start | bytes 1966080 | tf_op jit(solution)/shard_map/all_gather | solution.py:91
  142.8 101.5 %all-gather.8.cloned.1.call-start = ((), (), s32[]{:S(2)}) async-start(), calls=%async_computation | async-start | bytes 3538944 | tf_op jit(solution)/shard_map/all_gather | solution.py:84
  244.2 6.9 %copy-start.2 = (f32[49152]{0:T(1024)S(1)}, f32[49152]{0:T(1024)}, u32[]{:S(2)}) copy-start(f32[49152]{0:T(1024)} %all_gather.25) | copy-start | bytes 589828
  294.2 83.5 %copy-start.3 = (f32[49152]{0:T(1024)S(1)}, f32[49152]{0:T(1024)}, u32[]{:S(2)}) copy-start(f32[49152]{0:T(1024)} %all_gather.25) | copy-start | bytes 589828
  294.2 83.5 %copy-start.4 = (f32[49152,2]{0,1:T(2,128)S(1)}, f32[49152,2]{0,1:T(2,128)}, u32[]{:S(2)}) copy-start(f32[49152,2]{0,1:T(2,128)} %get-tuple-element.184) | copy-start | bytes 1179652
Sparse Core Ops, SparseCore 0:
  77.5 60.7 all-reduce.3
Sparse Core Ops, SparseCore 1:
  95.1 31.7 all-gather.11
  142.3 29.8 all-gather.9
  173.8 30.7 all-gather.13
  206.2 38.0 all-gather.7
where the time goes:
time: 389 us; the launch traced here: 387 us
  waiting for transfers between devices  105 us (27%)
  blocking collectives  87 us (22%)
  other arithmetic  73.1 us (19%)
  local copies, waits for them, and re-layouts  54.4 us (14%)
  matrix products  25.3 us (7%)
  loops' own time  22.7 us (6%)
  between operations  19.7 us (5%)
    convert_element_type x32, other arithmetic, unpack_half(): return bit_table.reshape(new_shape).astype(jnp.bfloat16)  55.2 us
    psum x1, waiting for transfers between devices, shards(): aon = lax.psum(partial_value, 'org')  42.7 us
    psum x1, blocking collectives, both_totals(): return lax.psum((cost_part, path_part), ('cls', 'org'))  39.7 us
    all_gather x1, waiting for transfers between devices, shards(): lax.all_gather(interaction, 'org', axis=2, tiled=True)  36 us
    all_gather x3, waiting for transfers between devices, full_cost(): flows_all = lax.all_gather(flow_value, 'cls', axis=0, tiled=True)  24.8 us
    dynamic_slice x32, local copies, waits for them, and re-layouts, fold_links(): lax.scan(advance, skim_carry, jnp.arange(turn_count, dtype=jnp.int32))  18.8 us
    all_gather x1, blocking collectives, shards(): lax.all_gather(flows_start, 'org', axis=1, tiled=True)  17.5 us
    shift_right_arithmetic x96, local copies, waits for them, and re-layouts, unpack_half(): jnp.right_shift(packed[..., :, None, :], shifts[:, None])  17.5 us
  transfers between devices with their start and end apart: 5, of which 3 were waited for; matrix products, arithmetic and copies ran while one was open for 4% of the time, Pallas kernels for 0%

commit v1 on v0

--- a/solution.py
+++ b/solution.py
@@ -88,7 +88,13 @@
     )
 
     def full_cost(flow_value):
-        flows_all = lax.all_gather(flow_value, "cls", axis=0, tiled=True)
+        size = lax.axis_size("cls")
+        held, pieces = (flow_value, [flow_value])
+        for _ in range(size - 1):
+            held = lax.ppermute(held, "cls", [(i, (i + 1) % size) for i in range(size)])
+            pieces.insert(0, held)
+        merged = jnp.concatenate(pieces, axis=0)
+        flows_all = jnp.roll(merged, (lax.axis_index("cls") + 1) * flow_value.shape[0], axis=0)
         return link_cost(flows_all, inter_full, free_full, cap_full)
 
     for iteration in range(ITERS):

time: 389 us -> 371 us (0.954)
  waiting for transfers between devices: 105 us -> 76.5 us
  other arithmetic: 73.1 us -> 85 us
  local copies, waits for them, and re-layouts: 54.4 us -> 44.9 us
  starting transfers between devices: 0.21 us -> 9.25 us
    all_gather x1, waiting for transfers between devices: 36 us -> 0.01 us  [shards(): lax.all_gather(interaction, 'org', axis=2, tiled=True)]
    ppermute x0 -> x9, waiting for transfers between devices: none -> 34.3 us  [full_cost(): held = lax.ppermute(held, 'cls', [(i, (i + 1) % size) for i in range(size)])]
    all_gather x3 -> x0, waiting for transfers between devices: 24.8 us -> none  [full_cost(): flows_all = lax.all_gather(flow_value, 'cls', axis=0, tiled=True)]
    unnamed x2 -> x5, other arithmetic: 0.01 us -> 12.9 us
    ppermute x0 -> x9, starting transfers between devices: none -> 9.17 us  [full_cost(): held = lax.ppermute(held, 'cls', [(i, (i + 1) % size) for i in range(size)])]
    unnamed x27 -> x42, local copies, waits for them, and re-layouts: 10.4 us -> 1.65 us
  transfers between devices with their start and end apart: 5 -> 11, of which waited for: 3 -> 6; matrix products, arithmetic and copies ran while one was open for 4% -> 5% of each run, Pallas kernels for 0% -> 0%
where the time goes in v1:
time: 371 us; the launch traced here: 370 us
  blocking collectives  88 us (24%)
  other arithmetic  85 us (23%)
  waiting for transfers between devices  76.5 us (21%)
  local copies, waits for them, and re-layouts  44.9 us (12%)
  matrix products  25.3 us (7%)
  loops' own time  22.7 us (6%)
  between operations  18.4 us (5%)
  starting transfers between devices  9.25 us (2%)
    convert_element_type x32, other arithmetic, unpack_half(): return bit_table.reshape(new_shape).astype(jnp.bfloat16)  55.2 us
    psum x1, waiting for transfers between devices, shards(): aon = lax.psum(partial_value, 'org')  42.1 us
    psum x1, blocking collectives, both_totals(): return lax.psum((cost_part, path_part), ('cls', 'org'))  38 us
    ppermute x9, waiting for transfers between devices, full_cost(): held = lax.ppermute(held, 'cls', [(i, (i + 1) % size) for i in range(size)])  34.3 us
    dynamic_slice x32, local copies, waits for them, and re-layouts, fold_links(): lax.scan(advance, skim_carry, jnp.arange(turn_count, dtype=jnp.int32))  18.8 us
    shift_right_arithmetic x96, local copies, waits for them, and re-layouts, unpack_half(): jnp.right_shift(packed[..., :, None, :], shifts[:, None])  17.5 us
    all_gather x1, blocking collectives, shards(): lax.all_gather(free_time, 'org', axis=1, tiled=True)  17.4 us
    all_gather x1, blocking collectives, shards(): lax.all_gather(flows_start, 'org', axis=1, tiled=True)  16.7 us
  transfers between devices with their start and end apart: 11, of which 6 were waited for; matrix products, arithmetic and copies ran while one was open for 5% of the time, Pallas kernels for 0%

profile of v1, /device:TPU:0, one launch (start us, length us, event | category | flops | bytes accessed | tf_op | source)
XLA Modules:
  0.0 370.1 jit_solution(3126476462378488224)
XLA Ops:
  10.1 32.3 %while.43 = (s32[]{:T(128)}, f32[8,2,6144]{2,1,0:T(2,128)S(1)}, s32[8]{0:T(128)S(1)}, s32[2,1,2,49152]{3,0,2,1:T(2,128)S(1)}, bf16[2,1,60]{2,0,1:T(2,128)(2,1)S(...) while((s32[]{:T(128)}, f32[8,2,6144]{2,1,0:T(2,128)S(1)}, s32[8]{0:T(128)S(1)}, ...), condition=%wide.region_4.5_spmd, body=%wide.region_3.4_spmd.sunk | while | flops 3686406 | bytes 3392847 | solution.py:46
  11.4 1.7 fusion.107
  15.5 1.7 fusion.107
  19.5 1.7 fusion.107
  23.5 1.7 fusion.107
  27.6 1.7 fusion.107
  31.6 1.7 fusion.107
  35.7 1.7 fusion.107
  39.7 1.7 fusion.107
  43.4 32.3 %while.42 = (s32[]{:T(128)}, f32[8,2,6144]{2,1,0:T(2,128)S(1)}, s32[8]{0:T(128)S(1)}, s32[2,1,2,49152]{3,0,2,1:T(2,128)S(1)}, bf16[2,1,60]{2,0,1:T(2,128)(2,1)S(...) while((s32[]{:T(128)}, f32[8,2,6144]{2,1,0:T(2,128)S(1)}, s32[8]{0:T(128)S(1)}, ...), condition=%wide.region_1.2_spmd, body=%wide.region_0.1_spmd.sunk | while | flops 3686406 | bytes 3392847 | solution.py:46
  44.7 1.7 fusion.103
  48.8 1.7 fusion.103
  52.8 1.7 fusion.103
  56.8 1.7 fusion.103
  60.9 1.7 fusion.103
  64.9 1.7 fusion.103
  68.9 1.7 fusion.103
  73.0 1.7 fusion.103
  76.5 16.7 %all_gather.12 = f32[2,49152]{1,0:T(2,128)S(1)} all-gather(f32[2,6144]{1,0:T(2,128)S(1)} %copy-done.16), channel_id=1, replica_groups=mesh['cls'=4,'org'=8] {'org'}, dimensions={1}, use_global_device_ids=true | all-gather | bytes 442368 | tf_op jit(solution)/shard_map/all_gather | solution.py:87
  95.2 42.1 %all-reduce.4.cloned.1.call-done = (f32[2,49152]{1,0:T(2,128)}, f32[2,49152]{1,0:T(2,128)}) async-done(((f32[2,49152]{1,0:T(2,128)}, f32[2,49152]{1,0:T(2,128)}), (f32[2,49152]{1,0:T(2,128)}, f32[2,49152]{1,0:T(2,128)})) %all-reduce.4.cloned.1.call-update) | async-done | bytes 786448 | tf_op jit(solution)/shard_map/psum | solution.py:105
  137.3 2.7 multiply_add_fusion
  144.6 16.0 %all_gather.15 = f32[49152]{0:T(1024)} all-gather(f32[6144]{0:T(1024)S(1)} %copy-done.18), channel_id=1, replica_groups=mesh['cls'=4,'org'=8] {'org'}, dimensions={0}, use_global_device_ids=true | all-gather | bytes 221184 | tf_op jit(solution)/shard_map/all_gather | solution.py:86
  160.6 17.4 %all_gather.13 = f32[2,49152]{1,0:T(2,128)} all-gather(f32[2,6144]{1,0:T(2,128)S(1)} %copy-done.17), channel_id=1, replica_groups=mesh['cls'=4,'org'=8] {'org'}, dimensions={1}, use_global_device_ids=true | all-gather | bytes 442368 | tf_op jit(solution)/shard_map/all_gather | solution.py:85
  181.9 9.0 %collective-permute-done.1 = f32[2,49152]{1,0:T(2,128)S(1)} collective-permute-done((f32[2,49152]{1,0:T(2,128)S(1)}, f32[2,49152]{1,0:T(2,128)S(1)}, u32[]{:S(2)}, u32[]{:S(2)}) %collective-permute-start.1) | collective-permute-done | bytes 393248 | tf_op jit(solution)/shard_map/ppermute | solution.py:94
  190.8 8.4 %collective-permute-done.7 = f32[2,49152]{1,0:T(2,128)S(1)} collective-permute-done((f32[2,49152]{1,0:T(2,128)S(1)}, f32[2,49152]{1,0:T(2,128)S(1)}, u32[]{:S(2)}, u32[]{:S(2)}) %collective-permute-start.7) | collective-permute-done | bytes 393248 | tf_op jit(solution)/shard_map/ppermute | solution.py:94
  199.3 8.4 %collective-permute-done.5 = f32[2,49152]{1,0:T(2,128)S(1)} collective-permute-done((f32[2,49152]{1,0:T(2,128)S(1)}, f32[2,49152]{1,0:T(2,128)S(1)}, u32[]{:S(2)}, u32[]{:S(2)}) %collective-permute-start.5) | collective-permute-done | bytes 393248 | tf_op jit(solution)/shard_map/ppermute | solution.py:94
  207.7 3.9 %fusion.56 = f32[49152,8]{0,1:T(8,128)S(1)} fusion(s32[]{:T(128)S(6)} %select_n.38, f32[2,49152]{1,0:T(2,128)S(1)} %collective-permute-done.5, f32[2,49152]{1,0:T(2,128)S(1)} %collective-permute-done.4, f32[2,49152]{1,0:T(2,128)S(1)} %collective-permute-done.3, f32[2,49152]{1,0:T(2,128)S(1)} %all_gather.12), kind=kLoop, calls=%fused_computation.97 | loop fusion | flops 2752512 | bytes 3145732
  211.6 4.5 %collective-permute-done.2 = f32[2,49152]{1,0:T(2,128)S(1)} collective-permute-done((f32[2,49152]{1,0:T(2,128)S(1)}, f32[2,49152]{1,0:T(2,128)S(1)}, u32[]{:S(2)}, u32[]{:S(2)}) %collective-permute-start.2) | collective-permute-done | bytes 393248 | tf_op jit(solution)/shard_map/ppermute | solution.py:94
  216.1 3.9 %fusion.64 = f32[49152,8]{0,1:T(8,128)S(1)} fusion(s32[]{:T(128)S(6)} %select_n.38, f32[2,49152]{1,0:T(2,128)S(1)} %collective-permute-done.2, f32[2,49152]{1,0:T(2,128)S(1)} %collective-permute-done.1, f32[2,49152]{1,0:T(2,128)S(1)} %copy-done.15, f32[2,49152]{1,0:T(2,128)S(1)} %copy-done.5), kind=kLoop, calls=%fused_computation.105 | loop fusion | flops 2752512 | bytes 3145732
  220.0 4.0 %collective-permute-done.8 = f32[2,49152]{1,0:T(2,128)S(1)} collective-permute-done((f32[2,49152]{1,0:T(2,128)S(1)}, f32[2,49152]{1,0:T(2,128)S(1)}, u32[]{:S(2)}, u32[]{:S(2)}) %collective-permute-start.8) | collective-permute-done | bytes 393248 | tf_op jit(solution)/shard_map/ppermute | solution.py:94
  224.0 5.2 %fusion.48 = f32[49152,8]{0,1:T(8,128)} fusion(s32[]{:T(128)S(6)} %select_n.38, f32[2,49152]{1,0:T(2,128)S(1)} %collective-permute-done.8, f32[2,49152]{1,0:T(2,128)S(1)} %collective-permute-done.7, f32[2,49152]{1,0:T(2,128)S(1)} %copy-done.13, f32[2,49152]{1,0:T(2,128)S(1)} %copy-done.3), kind=kLoop, calls=%fused_computation.89 | loop fusion | flops 2752512 | bytes 3145732
  229.2 6.9 %multiply_reduce_fusion.1 = (f32[49152,2]{0,1:T(2,128)S(1)}, f32[49152,2]{0,1:T(2,128)S(1)}, f32[49152,2]{0,1:T(2,128)}) fusion(f32[2,8,49152]{2,1,0:T(8,128)} %all-gather.2.cloned.1.call-done, f32[49152,8]{0,1:T(8,128)S(1)} %fusion.56, f32[49152,8]{0,1:T(8,128)} %fusion.48, f32[49152,8]{0,1:T(8,128)S(1)} %fusion.64), kind=kLoop, calls=%fused_computation.83 | loop fusion | flops 4423680 | bytes 9043968 | tf_op jit(solution)/shard_map/cel,el->cl/dot_general | solution.py:19
  237.6 39.4 %while.44 = (s32[]{:T(128)}, f32[2,1,60]{2,0,1:T(2,128)S(1)}, s32[8]{0:T(128)S(1)}, f32[2,49152]{1,0:T(2,128)S(1)}, s32[2,1,2,49152]{3,0,2,1:T(2,128)}, /*index=5*/s32[]{:T(128)}, s32[1]{0:T(128)}, s32[]{:T(128)}, s32[]{:T(128)}) while((s32[]{:T(128)}, f32[2,1,60]{2,0,1:T(2,128)S(1)}, s32[8]{0:T(128)S(1)}, ...), condition=%wide.region_8.10_spmd.clone, body=%wide.region_6.9_spmd.clone.sunk | while | flops 6943207 | bytes 3615725 | solution.py:62
  240.0 1.7 fusion.111
  245.0 1.7 fusion.111
  249.9 1.7 fusion.111
  254.8 1.7 fusion.111
  259.7 1.7 fusion.111
  264.7 1.7 fusion.111
  269.6 1.7 fusion.111
  274.5 1.7 fusion.111
  278.4 39.4 %while.45 = (s32[]{:T(128)}, f32[2,1,60]{2,0,1:T(2,128)S(1)}, s32[8]{0:T(128)S(1)}, f32[2,49152]{1,0:T(2,128)S(1)}, s32[2,1,2,49152]{3,0,2,1:T(2,128)}, /*index=5*/s32[]{:T(128)}, s32[1]{0:T(128)}, s32[]{:T(128)}, s32[]{:T(128)}) while((s32[]{:T(128)}, f32[2,1,60]{2,0,1:T(2,128)S(1)}, s32[8]{0:T(128)S(1)}, ...), condition=%wide.region_11.13_spmd.clone, body=%wide.region_9.12_spmd.clone.sunk | while | flops 6943207 | bytes 3615725 | solution.py:62
  280.9 1.7 fusion.117
  285.8 1.7 fusion.117
  290.7 1.7 fusion.117
  300.6 1.7 fusion.117
  305.5 1.7 fusion.117
  318.4 38.0 %all-reduce = (f32[]{:T(128)}, f32[]{:T(128)}, f32[]{:T(128)}, f32[]{:T(128)}) all-reduce(f32[]{:T(128)} %fusion.77, f32[]{:T(128)} %get-tuple-element.187, f32[]{:T(128)} %fusion.78, f32[]{:T(128)} %get-tuple-element.186), channel_id=1, replica_groups=mesh['cls'=4,'org'=8] {'cls','org'}, use_global_device_ids=true, to_apply=%region_17.19 | all-reduce | flops 4 | bytes 32 | tf_op jit(solution)/shard_map/psum | solution.py:69
  (356 shorter events, 92.0 us)
Async XLA Ops:
  7.2 130.1 %all-reduce.4.cloned.1.call-start = ((), (), s32[]{:S(2)}) async-start(), calls=%async_computation.1 | async-start | bytes 1572864 | tf_op jit(solution)/shard_map/psum | solution.py:105
  7.2 1.5 copy-start.20
  42.4 0.9 copy-start
  42.4 1.0 copy-start.11
  42.5 34.0 %copy-start.16 = (f32[2,6144]{1,0:T(2,128)S(1)}, f32[2,6144]{1,0:T(2,128)}, u32[]{:S(2)}) copy-start(f32[2,6144]{1,0:T(2,128)} %param.17) | copy-start | bytes 147460
  42.5 52.1 %copy-start.19 = (f32[2]{0:T(128)S(1)}, f32[2]{0:T(128)}, u32[]{:S(2)}) copy-start(f32[2]{0:T(128)} %param.23) | copy-start | bytes 28
  75.7 0.7 copy-start.10
  75.7 64.4 %copy-start.1 = (s32[2,1,2,49152]{3,0,2,1:T(2,128)}, s32[2,1,2,49152]{3,0,2,1:T(2,128)S(1)}, u32[]{:S(2)}) copy-start(s32[2,1,2,49152]{3,0,2,1:T(2,128)S(1)} %get-tuple-element.494) | copy-start | bytes 2359300
  76.4 68.2 %copy-start.18 = (f32[6144]{0:T(1024)S(1)}, f32[6144]{0:T(1024)}, u32[]{:S(2)}) copy-start(f32[6144]{0:T(1024)} %param.20) | copy-start | bytes 73732
  76.4 84.2 %copy-start.17 = (f32[2,6144]{1,0:T(2,128)S(1)}, f32[2,6144]{1,0:T(2,128)}, u32[]{:S(2)}) copy-start(f32[2,6144]{1,0:T(2,128)} %param.19) | copy-start | bytes 147460
  76.5 152.7 %all-gather.2.cloned.1.call-start = ((), (), s32[]{:S(2)}) async-start(), calls=%async_computation | async-start | bytes 3538944 | tf_op jit(solution)/shard_map/all_gather | solution.py:84
  93.2 49.9 %collective-permute-start.3 = (f32[2,49152]{1,0:T(2,128)S(1)}, f32[2,49152]{1,0:T(2,128)S(1)}, u32[]{:S(2)}, u32[]{:S(2)}) collective-permute-start(f32[2,49152]{1,0:T(2,128)S(1)} %all_gather.12), channel_id=1, source_target_pairs={{0,8},{8,16},{16,24},{24,0},{1,9},{9,17},{17,25},{25,1},{2,10},{10... | collective-permute-start | bytes 1179656 | tf_op jit(solution)/shard_map/ppermute | solution.py:94
  140.1 59.2 %copy-start.2 = (f32[2,49152]{1,0:T(2,128)}, f32[2,49152]{1,0:T(2,128)S(1)}, u32[]{:S(2)}) copy-start(f32[2,49152]{1,0:T(2,128)S(1)} %get-tuple-element.235) | copy-start | bytes 1179652
  140.1 59.2 %copy-start.4 = (f32[2,49152]{1,0:T(2,128)}, f32[2,49152]{1,0:T(2,128)S(1)}, u32[]{:S(2)}) copy-start(f32[2,49152]{1,0:T(2,128)S(1)} %get-tuple-element.234) | copy-start | bytes 1179652
  140.1 37.9 %collective-permute-start = (f32[2,49152]{1,0:T(2,128)S(1)}, f32[2,49152]{1,0:T(2,128)S(1)}, u32[]{:S(2)}, u32[]{:S(2)}) collective-permute-start(f32[2,49152]{1,0:T(2,128)S(1)} %get-tuple-element.234), channel_id=1, source_target_pairs={{0,8},{8,16},{16,24},{24,0},{1,9},{9,17},{17,25},{25,1},{2,10},{10... | collective-permute-start | bytes 1179656 | tf_op jit(solution)/shard_map/ppermute | solution.py:94
  141.6 36.7 %collective-permute-start.6 = (f32[2,49152]{1,0:T(2,128)S(1)}, f32[2,49152]{1,0:T(2,128)S(1)}, u32[]{:S(2)}, u32[]{:S(2)}) collective-permute-start(f32[2,49152]{1,0:T(2,128)S(1)} %get-tuple-element.235), channel_id=1, source_target_pairs={{0,8},{8,16},{16,24},{24,0},{1,9},{9,17},{17,25},{25,1},{2,10},{10... | collective-permute-start | bytes 1179656 | tf_op jit(solution)/shard_map/ppermute | solution.py:94
  143.1 36.7 %collective-permute-start.4 = (f32[2,49152]{1,0:T(2,128)S(1)}, f32[2,49152]{1,0:T(2,128)S(1)}, u32[]{:S(2)}, u32[]{:S(2)}) collective-permute-start(f32[2,49152]{1,0:T(2,128)S(1)} %collective-permute-done.3), channel_id=1, source_target_pairs={{0,8},{8,16},{16,24},{24,0},{1,9},{9,17},{17,25},{25,1},{2,10},{10... | collective-permute-start | bytes 1179656 | tf_op jit(solution)/shard_map/ppermute | solution.py:94
  178.0 21.3 %copy-start.14 = (f32[2,49152]{1,0:T(2,128)}, f32[2,49152]{1,0:T(2,128)S(1)}, u32[]{:S(2)}) copy-start(f32[2,49152]{1,0:T(2,128)S(1)} %collective-permute-done) | copy-start | bytes 1179652
  178.0 12.9 %collective-permute-start.1 = (f32[2,49152]{1,0:T(2,128)S(1)}, f32[2,49152]{1,0:T(2,128)S(1)}, u32[]{:S(2)}, u32[]{:S(2)}) collective-permute-start(f32[2,49152]{1,0:T(2,128)S(1)} %collective-permute-done), channel_id=1, source_target_pairs={{0,8},{8,16},{16,24},{24,0},{1,9},{9,17},{17,25},{25,1},{2,10},{10... | collective-permute-start | bytes 1179656 | tf_op jit(solution)/shard_map/ppermute | solution.py:94
  178.3 21.0 %copy-start.12 = (f32[2,49152]{1,0:T(2,128)}, f32[2,49152]{1,0:T(2,128)S(1)}, u32[]{:S(2)}) copy-start(f32[2,49152]{1,0:T(2,128)S(1)} %collective-permute-done.6) | copy-start | bytes 1179652
  178.3 21.0 %collective-permute-start.7 = (f32[2,49152]{1,0:T(2,128)S(1)}, f32[2,49152]{1,0:T(2,128)S(1)}, u32[]{:S(2)}, u32[]{:S(2)}) collective-permute-start(f32[2,49152]{1,0:T(2,128)S(1)} %collective-permute-done.6), channel_id=1, source_target_pairs={{0,8},{8,16},{16,24},{24,0},{1,9},{9,17},{17,25},{25,1},{2,10},{10... | collective-permute-start | bytes 1179656 | tf_op jit(solution)/shard_map/ppermute | solution.py:94
  179.8 27.9 %collective-permute-start.5 = (f32[2,49152]{1,0:T(2,128)S(1)}, f32[2,49152]{1,0:T(2,128)S(1)}, u32[]{:S(2)}, u32[]{:S(2)}) collective-permute-start(f32[2,49152]{1,0:T(2,128)S(1)} %collective-permute-done.4), channel_id=1, source_target_pairs={{0,8},{8,16},{16,24},{24,0},{1,9},{9,17},{17,25},{25,1},{2,10},{10... | collective-permute-start | bytes 1179656 | tf_op jit(solution)/shard_map/ppermute | solution.py:94
  190.8 25.3 %collective-permute-start.2 = (f32[2,49152]{1,0:T(2,128)S(1)}, f32[2,49152]{1,0:T(2,128)S(1)}, u32[]{:S(2)}, u32[]{:S(2)}) collective-permute-start(f32[2,49152]{1,0:T(2,128)S(1)} %collective-permute-done.1), channel_id=1, source_target_pairs={{0,8},{8,16},{16,24},{24,0},{1,9},{9,17},{17,25},{25,1},{2,10},{10... | collective-permute-start | bytes 1179656 | tf_op jit(solution)/shard_map/ppermute | solution.py:94
  199.3 24.7 %collective-permute-start.8 = (f32[2,49152]{1,0:T(2,128)S(1)}, f32[2,49152]{1,0:T(2,128)S(1)}, u32[]{:S(2)}, u32[]{:S(2)}) collective-permute-start(f32[2,49152]{1,0:T(2,128)S(1)} %collective-permute-done.7), channel_id=1, source_target_pairs={{0,8},{8,16},{16,24},{24,0},{1,9},{9,17},{17,25},{25,1},{2,10},{10... | collective-permute-start | bytes 1179656 | tf_op jit(solution)/shard_map/ppermute | solution.py:94
  207.7 8.4 %copy-start.5 = (f32[2,49152]{1,0:T(2,128)S(1)}, f32[2,49152]{1,0:T(2,128)}, u32[]{:S(2)}) copy-start(f32[2,49152]{1,0:T(2,128)} %copy-done.4) | copy-start | bytes 1179652
  207.7 8.4 %copy-start.15 = (f32[2,49152]{1,0:T(2,128)S(1)}, f32[2,49152]{1,0:T(2,128)}, u32[]{:S(2)}) copy-start(f32[2,49152]{1,0:T(2,128)} %copy-done.14) | copy-start | bytes 1179652
  211.6 12.4 %copy-start.3 = (f32[2,49152]{1,0:T(2,128)S(1)}, f32[2,49152]{1,0:T(2,128)}, u32[]{:S(2)}) copy-start(f32[2,49152]{1,0:T(2,128)} %copy-done.2) | copy-start | bytes 1179652
  211.6 12.4 %copy-start.13 = (f32[2,49152]{1,0:T(2,128)S(1)}, f32[2,49152]{1,0:T(2,128)}, u32[]{:S(2)}) copy-start(f32[2,49152]{1,0:T(2,128)} %copy-done.12) | copy-start | bytes 1179652
  229.2 6.9 %copy-start.6 = (f32[2,49152]{1,0:T(2,128)S(1)}, f32[2,49152]{1,0:T(2,128)}, u32[]{:S(2)}) copy-start(f32[2,49152]{1,0:T(2,128)} %all_gather.13) | copy-start | bytes 1179652
  229.2 6.9 %copy-start.7 = (f32[49152]{0:T(1024)S(1)}, f32[49152]{0:T(1024)}, u32[]{:S(2)}) copy-start(f32[49152]{0:T(1024)} %all_gather.15) | copy-start | bytes 589828
  278.4 82.0 %copy-start.8 = (f32[49152]{0:T(1024)S(1)}, f32[49152]{0:T(1024)}, u32[]{:S(2)}) copy-start(f32[49152]{0:T(1024)} %all_gather.15) | copy-start | bytes 589828
  278.4 82.0 %copy-start.9 = (f32[49152,2]{0,1:T(2,128)S(1)}, f32[49152,2]{0,1:T(2,128)}, u32[]{:S(2)}) copy-start(f32[49152,2]{0,1:T(2,128)} %get-tuple-element.185) | copy-start | bytes 1179652
Sparse Core Ops, SparseCore 0:
  76.5 60.7 all-reduce.3
  144.7 39.9 all-gather.1
